TPU v7x, 128 devices: a whole 4x4x4 slice. The times are simulated.
128 devices in a mesh: row: 16 (over y_hi, z, core), col: 8 (over y_lo, x).
Axes of the slice: x: 4, y: 4 (y_hi: 2, y_lo: 2; y = y_hi * 2 + y_lo), z: 4, core: 2. Of those that a mesh axis runs over, the one named last changes fastest.
Arguments:
- gate_input: bfloat16 [2, 1024, 53248], P(None, 'col', 'row'), may hold values from -6 to 6
- up_input: bfloat16 [2, 1024, 53248], P(None, 'col', 'row'), may hold values from -6 to 6
- down_weight: bfloat16 [53248, 16384], P('row', 'col'), may hold values from -0.02734375 to 0.02734375
Outputs:
- mixed: bfloat16 [2, 1024, 16384], P(None, 'row', 'col')
All inputs are finite; a program needn't handle non-finite values.
Results may differ from a plain program's by a relative error of at most 0.0049.
Values may be sent and summed in bfloat16 or wider, within the bound.
A program may use at most 128 MiB of HBM per device.

v0:
```python
import jax
import jax.numpy as jnp
from jax import lax
from jax.sharding import PartitionSpec as P


def gated_hidden(gate_part, up_part):
    product = jax.nn.silu(gate_part.astype(jnp.float32)) * up_part.astype(jnp.float32)
    return product.astype(jnp.bfloat16)


def gathered_hidden(gate_part, up_part):
    return lax.all_gather(gated_hidden(gate_part, up_part), "col", axis=1, tiled=True)


def body(gate_input, up_input, down_weight):
    hidden_units = down_weight.shape[0]
    width = down_weight.shape[1]
    hidden = gathered_hidden(gate_input, up_input)
    seq_count = hidden.shape[0]
    seq_tokens = hidden.shape[1]
    flat = hidden.reshape(seq_count * seq_tokens, hidden_units)
    partial_value = jnp.dot(flat, down_weight, preferred_element_type=jnp.float32)
    partial_value = partial_value.reshape(seq_count, seq_tokens, width)
    mixed = lax.psum_scatter(partial_value, "row", scatter_dimension=1, tiled=True)
    return mixed.astype(jnp.bfloat16)


def solution(mesh):
    return jax.shard_map(
        body,
        mesh=mesh,
        in_specs=(P(None, "col", "row"), P(None, "col", "row"), P("row", "col")),
        out_specs=P(None, "row", "col"),
        check_vma=False,
    )
```

profile of v0, /device:TPU:8, one launch (start us, length us, event | category | flops | bytes accessed | tf_op | source)
XLA Modules:
  0.0 344.0 jit_solution(2053406622738443245)
XLA Ops:
  6.5 0.0 all-gather.2.cloned.1.call-start
  6.5 4.2 %fusion.6 = bf16[2,128,3328]{2,1,0:T(8,128)(2,1)} fusion(bf16[2,128,3328]{2,1,0:T(8,128)(2,1)} %param.4, bf16[2,128,3328]{2,1,0:T(8,128)(2,1)} %param.3), kind=kLoop, calls=%fused_computation.8 | loop fusion | flops 6815744 | bytes 5111808 | tf_op jit(solution)/shard_map/convert_element_type | solution.py:9
  10.7 0.0 all-gather.2.cloned.1.call-update
  10.7 0.0 reduce-scatter.2.cloned.1.call-start
  10.8 142.4 %all-gather.2.cloned.1.call-done = bf16[2,1024,3328]{2,1,0:T(8,128)(2,1)} async-done(((bf16[2,128,3328]{2,1,0:T(8,128)(2,1)}), bf16[2,1024,3328]{2,1,0:T(8,128)(2,1)}) %all-gather.2.cloned.1.call-update) | async-done | bytes 13631504 | tf_op jit(solution)/shard_map/all_gather | solution.py:13
  153.2 35.6 %fusion = f32[2,1024,2048]{2,1,0:T(8,128)} fusion(bf16[2,1024,3328]{2,1,0:T(8,128)(2,1)} %all-gather.2.cloned.1.call-done, bf16[3328,2048]{1,0:T(8,128)(2,1)} %param.5), kind=kOutput, calls=%fused_computation | convolution fusion | flops 27917287424 | bytes 44040192 | tf_op jit(solution)/shard_map/dot_general | solution.py:23
  188.8 0.0 reduce-scatter.2.cloned.1.call-update
  188.9 146.3 %reduce-scatter.2.cloned.1.call-done = f32[2,64,2048]{2,1,0:T(8,128)} async-done(((f32[2,1024,2048]{2,1,0:T(8,128)}), f32[2,64,2048]{2,1,0:T(8,128)}) %reduce-scatter.2.cloned.1.call-update) | async-done | bytes 1048592 | tf_op jit(solution)/shard_map/reduce_scatter | solution.py:25
  335.1 2.1 convert_element_type.15
Async XLA Ops:
  6.5 146.7 %all-gather.2.cloned.1.call-start = ((), (), s32[]{:S(2)}) async-start(), calls=%async_computation.1 | async-start | bytes 15335424 | tf_op jit(solution)/shard_map/all_gather | solution.py:13
  10.7 324.4 %reduce-scatter.2.cloned.1.call-start = ((), (), s32[]{:S(2)}) async-start(), calls=%async_computation.2 | async-start | bytes 17825792 | tf_op jit(solution)/shard_map/reduce_scatter | solution.py:25
Sparse Core Ops, SparseCore 0:
  10.9 142.3 all-gather.1
  189.0 146.0 reduce-scatter.1
where the time goes:
time: 345 us; the launch traced here: 344 us
  waiting for transfers between devices  289 us (84%)
  matrix products  35.6 us (10%)
  between operations  13.4 us (4%)
  other arithmetic  6.26 us (2%)
    reduce_scatter x1, waiting for transfers between devices, body(): lax.psum_scatter(partial_value, 'row', scatter_dimension=1, tiled=True)  146 us
    all_gather x1, waiting for transfers between devices, gathered_hidden(): lax.all_gather(gated_hidden(gate_part, up_part), 'col', axis=1, tiled=True)  142 us
    dot_general x1, matrix products, body(): jnp.dot(flat, down_weight, preferred_element_type=jnp.float32)  35.6 us
  transfers between devices with their start and end apart: 2, of which 2 were waited for; matrix products, arithmetic and copies ran while one was open for 0% of the time, Pallas kernels for 0%

commit v1 on v0

v1 whole, which is shorter than its diff:
```python
import functools

import jax
import jax.numpy as jnp
from jax import lax
from jax.experimental import pallas as pl
from jax.experimental.pallas import tpu as pltpu
from jax.sharding import PartitionSpec as P

MESH = pl.DeviceIdType.MESH

BLOCKS = 8
ROWS = 16
AHEAD = 3
GROUP_SIZES = (8, 8, 8, 8, 8, 8, 4, 4, 4, 4)

PLUS = (
    [(0, 0, 0), (0, 0, 1), (0, 0, 2), (3, 0, 0), (0, 1, 3), (3, 0, 2), (0, 1, 4), (0, 1, 5), (0, 1, 6), (0, 1, 7)]
    + [(0, 0, 3), (0, 0, 4), (3, 1, 3), (0, 0, 5), (3, 1, 5), (0, 0, 6), (3, 0, 4), (0, 0, 7), (3, 1, 7, 0), (3, 0, 6)]
)
MINUS = (
    [(0, 0, 1), (0, 0, 0), (0, 0, 2), (1, 0, 1), (0, 1, 3), (0, 1, 4), (0, 1, 5), (0, 1, 6), (0, 1, 7), (0, 0, 3)]
    + [(0, 0, 4), (1, 1, 4), (0, 0, 5), (1, 1, 6), (1, 0, 3), (0, 0, 6), (0, 0, 7), (1, 0, 5), (1, 1, 7, 1), (1, 0, 7)]
)
ACROSS = (
    [(0, 0, 3), (0, 0, 4), (0, 0, 5), (0, 0, 6), (0, 0, 7), (0, 0, 0), (0, 0, 1), (0, 0, 2)]
    + [(3, 0, 0), (1, 0, 0), (3, 0, 1), (1, 0, 1), (3, 0, 2), (1, 0, 2), (2, 0, 0), (2, 0, 1), (2, 0, 2)]
)
OWN_ORDER = (0, 3, 1, 4, 2, 5, 6, 7)


def plan():
    links = []
    for items, shift_x, shift_y in ((PLUS, 3, 0), (MINUS, 1, 0), (ACROSS, 0, 1)):
        link = []
        for item in items:
            dx, dy, block = item[:3]
            half = item[3] if len(item) > 3 else None
            link.append(((dx, dy, block), half, ((dx + shift_x) % 4, dy ^ shift_y, block)))
        links.append(link)
    order = [(0, 0, b) for b in range(BLOCKS)]
    arrived_at = {key: -1 for key in order}
    slots = max(len(link) for link in links)
    for slot in range(slots):
        for link in links:
            if slot < len(link):
                key = link[slot][2]
                if key not in arrived_at:
                    order.append(key)
                arrived_at[key] = slot
    assert len(order) == 8 * BLOCKS
    for link in links:
        for slot, (source, _, _) in enumerate(link):
            assert arrived_at[source] <= slot - AHEAD or arrived_at[source] == -1
    groups, at = [], 0
    for size in GROUP_SIZES:
        groups.append(order[at : at + size])
        at += size
    assert at == len(order)
    place = {key: (g, q) for g, group in enumerate(groups) for q, key in enumerate(group)}
    start = [sum(GROUP_SIZES[:g]) for g in range(len(GROUP_SIZES))]
    ready = [max(arrived_at[key] for key in group) for group in groups]
    return links, groups, place, start, ready, slots


LINKS, GROUPS, PLACE, START, READY, SLOTS = plan()
N_GROUPS = len(GROUPS)
TILE_N = 512


def kernel(gate_ref, up_ref, weight_ref, out_ref, *scratch):
    hidden = scratch[:N_GROUPS]
    (gate_buf, up_buf, weight, result, halves, z_out, z_in, y_out, y_in) = scratch[N_GROUPS : N_GROUPS + 9]
    (load_sem, weight_sem, send_sem, recv_sem, pair_send, pair_recv, z_send, z_recv, y_send, y_recv) = scratch[N_GROUPS + 9 :]
    row = lax.axis_index("row")
    col = lax.axis_index("col")
    y_hi, z, core = row // 8, (row // 2) % 4, row % 2
    y_lo, x = col // 4, col % 4
    across = (row, (1 - y_lo) * 4 + x)
    plus = (row, y_lo * 4 + (x + 1) % 4)
    minus = (row, y_lo * 4 + (x + 3) % 4)
    partner = (y_hi * 8 + z * 2 + (1 - core), col)
    far = ((1 - y_hi) * 8 + z * 2 + core, col)
    targets = (plus, minus, across)
    root_dx = (z + 4 - x) % 4
    final_dy = (y_hi + y_lo) % 2

    def z_device(other):
        return (y_hi * 8 + other * 2 + core, col)

    barrier = pltpu.get_barrier_semaphore()
    for device in (plus, minus, across, partner, far, z_device((z + 1) % 4), z_device((z + 2) % 4), z_device((z + 3) % 4)):
        pl.semaphore_signal(barrier, inc=1, device_id=device, device_id_type=MESH)

    def load(block):
        s, j = divmod(block, 4)
        rows = pl.ds(j * ROWS, ROWS)
        return (
            pltpu.make_async_copy(gate_ref.at[s, :, rows, :], gate_buf.at[block], load_sem.at[0, block]),
            pltpu.make_async_copy(up_ref.at[s, :, rows, :], up_buf.at[block], load_sem.at[1, block]),
        )

    for block in OWN_ORDER:
        for copy in load(block):
            copy.start()
    weight_copy = pltpu.make_async_copy(weight_ref, weight, weight_sem)
    weight_copy.start()

    def view(key, half):
        g, q = PLACE[key]
        return hidden[g].at[:, q] if half is None else hidden[g].at[half, q]

    def transfer(link, slot):
        source, half, target = LINKS[link][slot]
        return pltpu.make_async_remote_copy(
            src_ref=view(source, half),
            dst_ref=view(target, half),
            send_sem=send_sem.at[link, slot],
            recv_sem=recv_sem.at[link, slot],
            device_id=targets[link],
            device_id_type=MESH,
        )

    greeted = False
    pending = [(link, slot) for slot in range(AHEAD) for link in range(3)]
    done = set()
    for block in OWN_ORDER:
        for copy in load(block):
            copy.wait()

        def gate_half(h, carry, block=block):
            gate = gate_buf[block, h].astype(jnp.float32)
            up = up_buf[block, h].astype(jnp.float32)
            hidden[0][h, block] = ((0.5 * gate) * (1.0 + jnp.tanh(0.5 * gate)) * up).astype(jnp.bfloat16)
            return carry

        lax.fori_loop(0, 2, gate_half, 0)
        if not greeted:
            pl.semaphore_wait(barrier, 8)
            greeted = True
        done.add(block)
        for link, slot in list(pending):
            if LINKS[link][slot][0][2] in done and not any(l == link and s < slot for l, s in pending):
                transfer(link, slot).start()
                pending.remove((link, slot))
    assert not pending
    weight_copy.wait()

    def pair_copy(g):
        size = GROUP_SIZES[g]
        return pltpu.make_async_remote_copy(
            src_ref=result.at[g % 2, 1 - core, pl.ds(0, size)],
            dst_ref=halves.at[pl.ds(START[g], size)],
            send_sem=pair_send.at[g],
            recv_sem=pair_recv.at[g],
            device_id=partner,
            device_id_type=MESH,
        )

    def z_copy(g, q):
        dx, dy, block = GROUPS[g][q]
        root = (x + dx) % 4
        offset = (z + 4 - root) % 4 - 1
        return root, pltpu.make_async_remote_copy(
            src_ref=z_out.at[START[g] + q],
            dst_ref=z_in.at[dy * BLOCKS + block, offset],
            send_sem=z_send.at[START[g] + q],
            recv_sem=z_recv.at[dy * BLOCKS + block, offset],
            device_id=z_device(root),
            device_id_type=MESH,
        )

    def z_arrival(dy, block, offset):
        return pltpu.make_async_remote_copy(
            src_ref=z_in.at[dy * BLOCKS + block, offset],
            dst_ref=z_in.at[dy * BLOCKS + block, offset],
            send_sem=z_send.at[0],
            recv_sem=z_recv.at[dy * BLOCKS + block, offset],
            device_id=z_device((z + 1) % 4),
            device_id_type=MESH,
        )

    def y_copy(dy, block):
        return pltpu.make_async_remote_copy(
            src_ref=y_out.at[dy * BLOCKS + block],
            dst_ref=y_in.at[block],
            send_sem=y_send.at[dy * BLOCKS + block],
            recv_sem=y_recv.at[block],
            device_id=far,
            device_id_type=MESH,
        )

    def multiply(g):
        size = GROUP_SIZES[g]
        if g >= 2:
            pair_copy(g - 2).wait_send()

        def tile(n, carry):
            columns = pl.ds(pl.multiple_of(n * TILE_N, TILE_N), TILE_N)
            left = hidden[g][...].reshape(size * 2 * ROWS, -1)
            value = jnp.dot(left, weight[:, columns], preferred_element_type=jnp.float32)
            result[g % 2, :, pl.ds(0, size), :, columns] = value.reshape(2, size, ROWS, TILE_N)
            return carry

        lax.fori_loop(0, weight.shape[1] // TILE_N, tile, 0)
        pair_copy(g).start()

    def add_pair(g):
        pair_copy(g).wait_recv()

        def one(q, carry):
            at = START[g] + q
            value = halves[at] + result[g % 2, core, q]
            halves[at] = value
            z_out[at] = value.astype(jnp.bfloat16)
            return carry

        lax.fori_loop(0, GROUP_SIZES[g], one, 0)
        for q in range(GROUP_SIZES[g]):
            root, copy = z_copy(g, q)

            @pl.when(root != z)
            def _():
                copy.start()

    def add_z(g):
        for q, (dx, dy, block) in enumerate(GROUPS[g]):
            at = START[g] + q

            @pl.when(root_dx == dx)
            def _():
                for offset in range(3):
                    z_arrival(dy, block, offset).wait_recv()

                def tile(n, carry):
                    columns = pl.ds(pl.multiple_of(n * TILE_N, TILE_N), TILE_N)
                    value = halves[at, :, columns]
                    for offset in range(3):
                        value = value + z_in[dy * BLOCKS + block, offset, :, columns].astype(jnp.float32)
                    halves[at, :, columns] = value
                    y_out[dy * BLOCKS + block, :, columns] = value.astype(jnp.bfloat16)
                    return carry

                lax.fori_loop(0, weight.shape[1] // TILE_N, tile, 0)

                @pl.when(final_dy != dy)
                def _():
                    y_copy(dy, block).start()

    def add_y(g):
        for q, (dx, dy, block) in enumerate(GROUPS[g]):
            at = START[g] + q
            s, j = divmod(block, 4)

            @pl.when((root_dx == dx) & (final_dy == dy))
            def _():
                y_copy(dy, block).wait_recv()

                def tile(n, carry):
                    columns = pl.ds(pl.multiple_of(n * TILE_N, TILE_N), TILE_N)
                    value = halves[at, :, columns] + y_in[block, :, columns].astype(jnp.float32)
                    out_ref[s, pl.ds(j * ROWS, ROWS), columns] = value.astype(jnp.bfloat16)
                    return carry

                lax.fori_loop(0, weight.shape[1] // TILE_N, tile, 0)

    def step(g):
        multiply(g)
        if g >= 1:
            add_pair(g - 1)
        if g >= 3:
            add_z(g - 3)
        if g >= 5:
            add_y(g - 5)

    step(0)
    for slot in range(SLOTS):
        for link in range(3):
            if slot < len(LINKS[link]):
                transfer(link, slot).wait_recv()
        for link in range(3):
            if slot + AHEAD < len(LINKS[link]):
                transfer(link, slot + AHEAD).start()
        for g in range(1, N_GROUPS):
            if READY[g] == slot:
                step(g)
    last = N_GROUPS - 1
    add_z(last - 2)
    add_pair(last)
    add_y(last - 4)
    add_z(last - 1)
    add_y(last - 3)
    add_z(last)
    for g in range(last - 2, last + 1):
        add_y(g)

    for link in range(3):
        for slot in range(len(LINKS[link])):
            transfer(link, slot).wait_send()
    pair_copy(last - 1).wait_send()
    pair_copy(last).wait_send()
    for g in range(N_GROUPS):
        for q in range(GROUP_SIZES[g]):
            root, copy = z_copy(g, q)

            @pl.when(root != z)
            def _():
                copy.wait_send()

    for dy in range(2):
        for block in range(BLOCKS):

            @pl.when(final_dy != dy)
            def _():
                y_copy(dy, block).wait_send()


def body(gate_input, up_input, down_weight):
    seqs, tokens, units = gate_input.shape
    width = down_weight.shape[1]
    halved = (seqs, 2, tokens // 2, units)
    bf16, f32 = jnp.bfloat16, jnp.float32
    dma = pltpu.SemaphoreType.DMA
    any_spec = pl.BlockSpec(memory_space=pl.ANY)
    return pl.pallas_call(
        kernel,
        out_shape=jax.ShapeDtypeStruct((seqs, tokens // 2, width), bf16),
        in_specs=[any_spec, any_spec, any_spec],
        out_specs=pl.BlockSpec(memory_space=pltpu.VMEM),
        scratch_shapes=[
            *[pltpu.VMEM((2, size, ROWS, units), bf16) for size in GROUP_SIZES],
            pltpu.VMEM((BLOCKS, 2, ROWS, units), bf16),
            pltpu.VMEM((BLOCKS, 2, ROWS, units), bf16),
            pltpu.VMEM((units, width), bf16),
            pltpu.VMEM((2, 2, BLOCKS, ROWS, width), f32),
            pltpu.VMEM((8 * BLOCKS, ROWS, width), f32),
            pltpu.VMEM((8 * BLOCKS, ROWS, width), bf16),
            pltpu.VMEM((2 * BLOCKS, 3, ROWS, width), bf16),
            pltpu.VMEM((2 * BLOCKS, ROWS, width), bf16),
            pltpu.VMEM((BLOCKS, ROWS, width), bf16),
            dma((2, BLOCKS)),
            dma,
            dma((3, SLOTS)),
            dma((3, SLOTS)),
            dma((N_GROUPS,)),
            dma((N_GROUPS,)),
            dma((8 * BLOCKS,)),
            dma((2 * BLOCKS, 3)),
            dma((2 * BLOCKS,)),
            dma((BLOCKS,)),
        ],
        compiler_params=pltpu.CompilerParams(
            collective_id=0, has_side_effects=True, vmem_limit_bytes=63 * 1024 * 1024
        ),
    )(gate_input.reshape(halved), up_input.reshape(halved), down_weight)


def solution(mesh):
    return jax.shard_map(
        body,
        mesh=mesh,
        in_specs=(P(None, "col", "row"), P(None, "col", "row"), P("row", "col")),
        out_specs=P(None, "row", "col"),
        check_vma=False,
    )
```

time: 345 us -> 131 us (0.38)
  the two profiles are of different devices: /device:TPU:8 before, /device:TPU:46 now
where the time goes in v1:
time: 131 us
  Pallas kernels  129 us (98%)
  local copies, waits for them, and re-layouts  1.88 us (1%)
    pallas_call x1, Pallas kernels, body(): pl.pallas_call(kernel, out_shape=jax.ShapeDtypeStruct((seqs, tokens // 2,...  129 us

profile of v1, /device:TPU:46, one launch (start us, length us, event | category | flops | bytes accessed | tf_op | source)
XLA Modules:
  0.0 131.3 jit_solution(13664636338102035520)
XLA Ops:
  0.0 129.4 %shard_map.37 = bf16[2,64,2048]{2,1,0:T(8,128)(2,1)} custom-call(bf16[2,2,64,3328]{3,2,1,0:T(8,128)(2,1)} %bitcast.2, bf16[2,2,64,3328]{3,2,1,0:T(8,128)(2,1)} %bitcast.3, bf16[3328,2048]{1,0:T(8,128)(2,1)} %weight_ref.1), custom_call_target="tpu_custom_call" | custom-call | tf_op jit(solution)/shard_map/pallas_call | solution.py:325
  129.4 1.9 %copy.5 = bf16[2,64,2048]{2,1,0:T(8,128)(2,1)} copy(bf16[2,64,2048]{2,1,0:T(8,128)(2,1)} %shard_map.37) | data formatting | bytes 1048576

commit v2 on v1

v2 whole, which is shorter than its diff:
```python
import functools

import jax
import jax.numpy as jnp
from jax import lax
from jax.experimental import pallas as pl
from jax.experimental.pallas import tpu as pltpu
from jax.sharding import PartitionSpec as P

MESH = pl.DeviceIdType.MESH

BLOCKS = 8
ROWS = 16
AHEAD = 3
GROUP_SIZES = (8, 6, 6, 6, 6, 5, 6, 4, 6, 6, 2, 3)
LAST = len(GROUP_SIZES) - 1
PARTS = 2

PLUS = (
    [(0, 0, 0), (0, 0, 2), (0, 0, 1), (3, 0, 0), (0, 1, 3), (3, 0, 2), (0, 1, 5), (3, 1, 3), (0, 0, 4), (0, 1, 7)]
    + [(3, 1, 5), (3, 0, 4), (0, 0, 6), (3, 1, 7, 0), (0, 0, 3), (3, 0, 6), (0, 1, 4), (0, 0, 5), (0, 1, 6), (0, 0, 7)]
)
MINUS = (
    [(0, 0, 1), (0, 0, 0), (0, 0, 3), (1, 0, 1), (0, 1, 4), (1, 0, 3), (0, 1, 6), (1, 1, 4), (0, 0, 5), (0, 1, 7)]
    + [(1, 1, 6), (1, 0, 5), (0, 0, 7), (1, 1, 7, 1), (0, 0, 2), (1, 0, 7), (0, 1, 3), (0, 0, 4), (0, 1, 5), (0, 0, 6)]
)
ACROSS = (
    [(0, 0, 3), (0, 0, 4), (0, 0, 5), (0, 0, 6), (0, 0, 7), (3, 0, 0), (1, 0, 1), (2, 0, 0), (2, 0, 1), None]
    + [(1, 0, 0), (2, 0, 2), (3, 0, 2), None, (3, 0, 1), (0, 0, 0), (0, 0, 1), (1, 0, 2), None, (0, 0, 2)]
)
OWN_ORDER = (0, 1, 3, 2, 4, 5, 6, 7)


def plan():
    links = []
    for items, shift_x, shift_y in ((PLUS, 3, 0), (MINUS, 1, 0), (ACROSS, 0, 1)):
        link = []
        for item in items:
            if item is None:
                link.append(None)
                continue
            dx, dy, block = item[:3]
            half = item[3] if len(item) > 3 else None
            link.append(((dx, dy, block), half, ((dx + shift_x) % 4, dy ^ shift_y, block)))
        links.append(link)
    order = [(0, 0, b) for b in range(BLOCKS)]
    arrived_at = {key: -1 for key in order}
    slots = max(len(link) for link in links)
    for slot in range(slots):
        for link in links:
            if slot < len(link) and link[slot]:
                key = link[slot][2]
                if key not in arrived_at:
                    order.append(key)
                arrived_at[key] = slot
    assert len(order) == 8 * BLOCKS
    issue = {}
    for link in links:
        for slot, item in enumerate(link):
            source = item[0] if item else order[0]
            issue.setdefault(max(arrived_at[source], slot - AHEAD, -1), []).append((links.index(link), slot))
    groups, at = [], 0
    for size in GROUP_SIZES:
        groups.append(sorted(order[at : at + size]))
        at += size
    assert at == len(order)
    place = {key: (g, q) for g, group in enumerate(groups) for q, key in enumerate(group)}
    start = [sum(GROUP_SIZES[:g]) for g in range(len(GROUP_SIZES))]
    ready = [max(arrived_at[key] for key in group) for group in groups]
    return links, groups, place, start, ready, slots, issue


LINKS, GROUPS, PLACE, START, READY, SLOTS, ISSUE = plan()
N_GROUPS = len(GROUPS)
UNITS = [(g, 0) for g in range(LAST)] + [(LAST, part) for part in range(PARTS)]
TILE_N = 512


def runs_of(g):
    runs = []
    for dx in range(4):
        places = [q for q, key in enumerate(GROUPS[g]) if key[0] == dx]
        if places:
            rank = sum(key[0] == dx for group in GROUPS[:g] for key in group)
            runs.append((dx, places[0], len(places), rank))
    return runs


def y_runs_of(g, dx):
    runs = []
    for dy in range(2):
        places = [q for q, key in enumerate(GROUPS[g]) if key[:2] == (dx, dy)]
        if places:
            rank = sum(key[:2] == (dx, dy) for group in GROUPS[:g] for key in group)
            runs.append((dy, places[0], len(places), rank))
    return runs


def kernel(gate_ref, up_ref, weight_ref, out_ref, *scratch):
    hidden = scratch[:N_GROUPS]
    (gate_buf, up_buf, weight, result, halves, z_out, z_in, y_out, y_in) = scratch[N_GROUPS : N_GROUPS + 9]
    last_bufs = scratch[N_GROUPS + 9 : N_GROUPS + 15]
    (load_sem, weight_sem, send_sem, recv_sem, pair_send, pair_recv, z_send, z_recv, y_send, y_recv) = scratch[N_GROUPS + 15 :]
    result_last, halves_last, z_out_last, z_in_last, y_out_last, y_in_last = last_bufs
    row = lax.axis_index("row")
    col = lax.axis_index("col")
    y_hi, z, core = row // 8, (row // 2) % 4, row % 2
    y_lo, x = col // 4, col % 4
    across = (row, (1 - y_lo) * 4 + x)
    plus = (row, y_lo * 4 + (x + 1) % 4)
    minus = (row, y_lo * 4 + (x + 3) % 4)
    partner = (y_hi * 8 + z * 2 + (1 - core), col)
    far = ((1 - y_hi) * 8 + z * 2 + core, col)
    targets = (plus, minus, across)
    root_dx = (z + 4 - x) % 4
    final_dy = (y_hi + y_lo) % 2

    def z_device(other):
        return (y_hi * 8 + other * 2 + core, col)

    barrier = pltpu.get_barrier_semaphore()
    for device in (plus, minus, across, partner, far, z_device((z + 1) % 4), z_device((z + 2) % 4), z_device((z + 3) % 4)):
        pl.semaphore_signal(barrier, inc=1, device_id=device, device_id_type=MESH)

    def load(block):
        s, j = divmod(block, 4)
        rows = pl.ds(j * ROWS, ROWS)
        return (
            pltpu.make_async_copy(gate_ref.at[s, :, rows, :], gate_buf.at[block], load_sem.at[0, block]),
            pltpu.make_async_copy(up_ref.at[s, :, rows, :], up_buf.at[block], load_sem.at[1, block]),
        )

    for block in OWN_ORDER:
        for copy in load(block):
            copy.start()
    weight_copy = pltpu.make_async_copy(weight_ref, weight, weight_sem)
    weight_copy.start()

    def view(key, half):
        g, q = PLACE[key]
        return hidden[g].at[q] if half is None else hidden[g].at[q, half]

    def transfer(link, slot):
        source, half, target = LINKS[link][slot]
        return pltpu.make_async_remote_copy(
            src_ref=view(source, half),
            dst_ref=view(target, half),
            send_sem=send_sem.at[link, slot],
            recv_sem=recv_sem.at[link, slot],
            device_id=targets[link],
            device_id_type=MESH,
        )

    greeted = False
    pending = sorted((i for i in ISSUE[-1] if LINKS[i[0]][i[1]]), key=lambda i: i[1])
    done = set()
    for block in OWN_ORDER:
        for copy in load(block):
            copy.wait()

        def gate_half(h, carry, block=block):
            gate = gate_buf[block, h].astype(jnp.float32)
            up = up_buf[block, h].astype(jnp.float32)
            hidden[0][block, h] = ((0.5 * gate) * (1.0 + jnp.tanh(0.5 * gate)) * up).astype(jnp.bfloat16)
            return carry

        lax.fori_loop(0, 2, gate_half, 0)
        if not greeted:
            pl.semaphore_wait(barrier, 8)
            greeted = True
        done.add(block)
        for link, slot in list(pending):
            if LINKS[link][slot][0][2] in done and not any(l == link and s < slot for l, s in pending):
                transfer(link, slot).start()
                pending.remove((link, slot))
    assert not pending
    weight_copy.wait()
    width = weight.shape[1]

    def sums(g, part):
        return halves_last.at[part] if g == LAST else halves.at[pl.ds(START[g], GROUP_SIZES[g])]

    def outgoing(g, part):
        return z_out_last.at[part] if g == LAST else z_out.at[pl.ds(START[g], GROUP_SIZES[g])]

    def products(g, part, half):
        return result_last.at[part, half] if g == LAST else result.at[g % 2, half, pl.ds(0, GROUP_SIZES[g])]

    def z_landing(g, part, offset, run):
        _, first, count, rank = run
        return z_in_last.at[part, offset, pl.ds(first, count)] if g == LAST else z_in.at[offset, pl.ds(rank, count)]

    def y_leaving(g, part, run, y_run):
        _, z_first, _, rank = run
        _, first, count, _ = y_run
        if g == LAST:
            return y_out_last.at[part, pl.ds(first, count)]
        return y_out.at[pl.ds(rank + first - z_first, count)]

    def y_landing(g, part, y_run):
        _, first, count, rank = y_run
        return y_in_last.at[part, pl.ds(first, count)] if g == LAST else y_in.at[pl.ds(rank, count)]

    def remote(source, target, sent, received, device):
        return pltpu.make_async_remote_copy(
            src_ref=source, dst_ref=target, send_sem=sent, recv_sem=received, device_id=device, device_id_type=MESH
        )

    def pair_copy(g, part):
        unit = g + part
        return remote(products(g, part, 1 - core), sums(g, part), pair_send.at[unit], pair_recv.at[unit], partner)

    def z_copy(g, part, run):
        dx, first, count, _ = run
        root = (x + dx) % 4
        offset = (z + 4 - root) % 4 - 1
        unit = g + part
        source = outgoing(g, part).at[pl.ds(first, count)]
        return root, remote(
            source, z_landing(g, part, offset, run), z_send.at[unit, dx], z_recv.at[unit, offset], z_device(root)
        )

    def z_arrival(g, part, offset, run):
        landed = z_landing(g, part, offset, run)
        return remote(landed, landed, z_send.at[0, 0], z_recv.at[g + part, offset], z_device((z + 1) % 4))

    def y_copy(g, part, run, y_run):
        unit = g + part
        return remote(y_leaving(g, part, run, y_run), y_landing(g, part, y_run), y_send.at[unit], y_recv.at[unit], far)

    def multiply(g, part):
        size = GROUP_SIZES[g]
        span = width // PARTS if g == LAST else width

        def tile(n, carry):
            columns = pl.ds(pl.multiple_of(n * TILE_N, TILE_N), TILE_N)
            taken = pl.ds(pl.multiple_of(n * TILE_N + part * span, TILE_N), TILE_N)
            left = hidden[g][...].reshape(size * 2 * ROWS, -1)
            value = jnp.dot(left, weight[:, taken], preferred_element_type=jnp.float32)
            value = value.reshape(size, 2, ROWS, TILE_N)
            for half in range(2):
                products(g, part, half)[:, :, columns] = value[:, half]
            return carry

        lax.fori_loop(0, span // TILE_N, tile, 0)
        pair_copy(g, part).start()

    def tiles(count, span, body):
        steps = span // TILE_N

        def one(i, carry):
            body(i // steps, pl.ds(pl.multiple_of(i % steps * TILE_N, TILE_N), TILE_N))
            return carry

        lax.fori_loop(0, count * steps, one, 0)

    def add_pair(g, part):
        pair_copy(g, part).wait_recv()
        own, total, out = products(g, part, core), sums(g, part), outgoing(g, part)

        def add(q, columns):
            value = total[q, :, columns] + own[q, :, columns]
            total[q, :, columns] = value
            out[q, :, columns] = value.astype(jnp.bfloat16)

        tiles(GROUP_SIZES[g], total.shape[-1], add)
        for run in runs_of(g):
            root, copy = z_copy(g, part, run)

            @pl.when(root != z)
            def _():
                copy.start()

        pair_copy(g, part).wait_send()

    def add_z(g, part=0):
        for run in runs_of(g):
            dx, first, count, _ = run

            @pl.when(root_dx == dx)
            def _():
                total = sums(g, part)
                for offset in range(3):
                    z_arrival(g, part, offset, run).wait_recv()
                for y_run in y_runs_of(g, dx):
                    dy, y_first, y_count, _ = y_run
                    leaving = y_leaving(g, part, run, y_run)

                    def add(q, columns):
                        value = total[y_first + q, :, columns]
                        for offset in range(3):
                            landed = z_landing(g, part, offset, run)
                            value = value + landed[y_first - first + q, :, columns].astype(jnp.float32)
                        total[y_first + q, :, columns] = value
                        leaving[q, :, columns] = value.astype(jnp.bfloat16)

                    tiles(y_count, total.shape[-1], add)

                    @pl.when(final_dy != dy)
                    def _():
                        y_copy(g, part, run, y_run).start()

    def add_y(g, part=0):
        for run in runs_of(g):
            dx = run[0]
            for y_run in y_runs_of(g, dx):
                dy, y_first, y_count, _ = y_run

                @pl.when((root_dx == dx) & (final_dy == dy))
                def _():
                    total, landed = sums(g, part), y_landing(g, part, y_run)
                    span = total.shape[-1]
                    y_copy(g, part, run, y_run).wait_recv()
                    for q in range(y_count):
                        s, j = divmod(GROUPS[g][y_first + q][2], 4)

                        def add(_, columns):
                            value = total[y_first + q, :, columns] + landed[q, :, columns].astype(jnp.float32)
                            taken = pl.ds(pl.multiple_of(columns.start + part * span, TILE_N), TILE_N)
                            out_ref[s, pl.ds(j * ROWS, ROWS), taken] = value.astype(jnp.bfloat16)

                        tiles(1, span, add)

    z_work = {4: (0, 1), 5: (2,), 6: (3,), 7: (4,), 8: (5,), 9: (6,), 10: (7,)}
    y_work = {7: (0, 1), 8: (2,), 9: (3,), 10: (4,)}

    def step(g):
        multiply(g, 0)
        for older in z_work.get(g, ()):
            add_z(older)
        for older in y_work.get(g, ()):
            add_y(older)
        add_pair(g, 0)

    def last_step():
        multiply(LAST, 0)
        add_z(LAST - 3)
        multiply(LAST, 1)
        add_pair(LAST, 0)
        add_pair(LAST, 1)
        add_y(LAST - 6)
        add_z(LAST - 2)
        add_z(LAST - 1)
        add_y(LAST - 5)
        add_z(LAST, 0)
        add_y(LAST - 4)
        add_z(LAST, 1)
        for g in range(LAST - 3, LAST):
            add_y(g)
        add_y(LAST, 0)
        add_y(LAST, 1)

    step(0)
    for slot in range(SLOTS):
        for link in range(3):
            if LINKS[link][slot]:
                transfer(link, slot).wait_recv()
        for link, later in sorted(ISSUE.get(slot, ()), key=lambda i: i[1]):
            if LINKS[link][later]:
                transfer(link, later).start()
        for g in range(1, N_GROUPS):
            if READY[g] == slot:
                step(g) if g < LAST else last_step()

    for link in range(3):
        for slot in range(SLOTS):
            if LINKS[link][slot]:
                transfer(link, slot).wait_send()
    for g, part in UNITS:
        for run in runs_of(g):
            root, copy = z_copy(g, part, run)

            @pl.when(root != z)
            def _():
                copy.wait_send()

            for y_run in y_runs_of(g, run[0]):

                @pl.when((root_dx == run[0]) & (final_dy != y_run[0]))
                def _():
                    y_copy(g, part, run, y_run).wait_send()


def body(gate_input, up_input, down_weight):
    seqs, tokens, units = gate_input.shape
    width = down_weight.shape[1]
    halved = (seqs, 2, tokens // 2, units)
    bf16, f32 = jnp.bfloat16, jnp.float32
    dma = pltpu.SemaphoreType.DMA
    last, part_width = GROUP_SIZES[LAST], width // PARTS
    earlier = 8 * BLOCKS - last
    any_spec = pl.BlockSpec(memory_space=pl.ANY)
    return pl.pallas_call(
        kernel,
        out_shape=jax.ShapeDtypeStruct((seqs, tokens // 2, width), bf16),
        in_specs=[any_spec, any_spec, any_spec],
        out_specs=pl.BlockSpec(memory_space=pltpu.VMEM),
        scratch_shapes=[
            *[pltpu.VMEM((size, 2, ROWS, units), bf16) for size in GROUP_SIZES],
            pltpu.VMEM((BLOCKS, 2, ROWS, units), bf16),
            pltpu.VMEM((BLOCKS, 2, ROWS, units), bf16),
            pltpu.VMEM((units, width), bf16),
            pltpu.VMEM((2, 2, BLOCKS, ROWS, width), f32),
            pltpu.VMEM((earlier, ROWS, width), f32),
            pltpu.VMEM((earlier, ROWS, width), bf16),
            pltpu.VMEM((3, 2 * BLOCKS, ROWS, width), bf16),
            pltpu.VMEM((2 * BLOCKS, ROWS, width), bf16),
            pltpu.VMEM((BLOCKS, ROWS, width), bf16),
            pltpu.VMEM((PARTS, 2, last, ROWS, part_width), f32),
            pltpu.VMEM((PARTS, last, ROWS, part_width), f32),
            pltpu.VMEM((PARTS, last, ROWS, part_width), bf16),
            pltpu.VMEM((PARTS, 3, last, ROWS, part_width), bf16),
            pltpu.VMEM((PARTS, last, ROWS, part_width), bf16),
            pltpu.VMEM((PARTS, last, ROWS, part_width), bf16),
            dma((2, BLOCKS)),
            dma,
            dma((3, SLOTS)),
            dma((3, SLOTS)),
            dma((len(UNITS),)),
            dma((len(UNITS),)),
            dma((len(UNITS), 4)),
            dma((len(UNITS), 3)),
            dma((len(UNITS),)),
            dma((len(UNITS),)),
        ],
        compiler_params=pltpu.CompilerParams(
            collective_id=0, has_side_effects=True, vmem_limit_bytes=63 * 1024 * 1024
        ),
    )(gate_input.reshape(halved), up_input.reshape(halved), down_weight)


def solution(mesh):
    return jax.shard_map(
        body,
        mesh=mesh,
        in_specs=(P(None, "col", "row"), P(None, "col", "row"), P("row", "col")),
        out_specs=P(None, "row", "col"),
        check_vma=False,
    )
```

time: 131 us -> 121 us (0.924)
  the two profiles are of different devices: /device:TPU:46 before, /device:TPU:15 now
where the time goes in v2:
time: 121 us
  Pallas kernels  119 us (98%)
  local copies, waits for them, and re-layouts  1.88 us (2%)
    pallas_call x1, Pallas kernels, body(): pl.pallas_call(kernel, out_shape=jax.ShapeDtypeStruct((seqs, tokens // 2,...  119 us

profile of v2, /device:TPU:15, one launch (start us, length us, event | category | flops | bytes accessed | tf_op | source)
XLA Modules:
  0.0 121.1 jit_solution(3860271750344388620)
XLA Ops:
  0.0 119.2 %shard_map.37 = bf16[2,64,2048]{2,1,0:T(8,128)(2,1)} custom-call(bf16[2,2,64,3328]{3,2,1,0:T(8,128)(2,1)} %bitcast.2, bf16[2,2,64,3328]{3,2,1,0:T(8,128)(2,1)} %bitcast.3, bf16[3328,2048]{1,0:T(8,128)(2,1)} %weight_ref.1), custom_call_target="tpu_custom_call" | custom-call | tf_op jit(solution)/shard_map/pallas_call | solution.py:393
  119.2 1.9 %copy.5 = bf16[2,64,2048]{2,1,0:T(8,128)(2,1)} copy(bf16[2,64,2048]{2,1,0:T(8,128)(2,1)} %shard_map.37) | data formatting | bytes 1048576

commit v3 on v2

--- a/solution.py
+++ b/solution.py
@@ -12,21 +12,21 @@
 BLOCKS = 8
 ROWS = 16
 AHEAD = 3
-GROUP_SIZES = (8, 6, 6, 6, 6, 5, 6, 4, 6, 6, 2, 3)
+GROUP_SIZES = (8, 6, 6, 6, 6, 5, 6, 4, 6, 3, 3, 2, 3)
 LAST = len(GROUP_SIZES) - 1
-PARTS = 2
+PARTS = 4
 
 PLUS = (
     [(0, 0, 0), (0, 0, 2), (0, 0, 1), (3, 0, 0), (0, 1, 3), (3, 0, 2), (0, 1, 5), (3, 1, 3), (0, 0, 4), (0, 1, 7)]
     + [(3, 1, 5), (3, 0, 4), (0, 0, 6), (3, 1, 7, 0), (0, 0, 3), (3, 0, 6), (0, 1, 4), (0, 0, 5), (0, 1, 6), (0, 0, 7)]
 )
 MINUS = (
-    [(0, 0, 1), (0, 0, 0), (0, 0, 3), (1, 0, 1), (0, 1, 4), (1, 0, 3), (0, 1, 6), (1, 1, 4), (0, 0, 5), (0, 1, 7)]
-    + [(1, 1, 6), (1, 0, 5), (0, 0, 7), (1, 1, 7, 1), (0, 0, 2), (1, 0, 7), (0, 1, 3), (0, 0, 4), (0, 1, 5), (0, 0, 6)]
+    [(0, 0, 1), (0, 0, 0), (0, 0, 3), (1, 0, 1), (0, 1, 4), (1, 0, 3), (0, 1, 6), (1, 1, 4), (0, 0, 2), (0, 1, 7)]
+    + [(1, 1, 6), (0, 0, 5), (0, 0, 7), (1, 1, 7, 1), (1, 0, 5), (1, 0, 7), (0, 1, 3), (0, 0, 4), (0, 1, 5), (0, 0, 6)]
 )
 ACROSS = (
     [(0, 0, 3), (0, 0, 4), (0, 0, 5), (0, 0, 6), (0, 0, 7), (3, 0, 0), (1, 0, 1), (2, 0, 0), (2, 0, 1), None]
-    + [(1, 0, 0), (2, 0, 2), (3, 0, 2), None, (3, 0, 1), (0, 0, 0), (0, 0, 1), (1, 0, 2), None, (0, 0, 2)]
+    + [(1, 0, 0), (2, 0, 2), (3, 0, 2), None, (1, 0, 2), (3, 0, 1), (0, 0, 0), (0, 0, 1), None, (0, 0, 2)]
 )
 OWN_ORDER = (0, 1, 3, 2, 4, 5, 6, 7)
 
@@ -151,7 +151,6 @@
             device_id_type=MESH,
         )
 
-    greeted = False
     pending = sorted((i for i in ISSUE[-1] if LINKS[i[0]][i[1]]), key=lambda i: i[1])
     done = set()
     for block in OWN_ORDER:
@@ -165,10 +164,11 @@
             return carry
 
         lax.fori_loop(0, 2, gate_half, 0)
-        if not greeted:
+        done.add(block)
+        if len(done) < 3:
+            continue
+        if len(done) == 3:
             pl.semaphore_wait(barrier, 8)
-            greeted = True
-        done.add(block)
         for link, slot in list(pending):
             if LINKS[link][slot][0][2] in done and not any(l == link and s < slot for l, s in pending):
                 transfer(link, slot).start()
@@ -321,34 +321,41 @@
 
                         tiles(1, span, add)
 
-    z_work = {4: (0, 1), 5: (2,), 6: (3,), 7: (4,), 8: (5,), 9: (6,), 10: (7,)}
-    y_work = {7: (0, 1), 8: (2,), 9: (3,), 10: (4,)}
+    z_work = {4: (0, 1), 5: (2,), 6: (3,), 7: (4,), 8: (5,), 9: (6,), 10: (7,), 11: (8,)}
+    y_work = {7: (0, 1), 8: (2,), 9: (3,), 10: (4,), 11: (5,)}
 
     def step(g):
+        if g > 9:
+            add_pair(g - 1, 0)
         multiply(g, 0)
         for older in z_work.get(g, ()):
             add_z(older)
         for older in y_work.get(g, ()):
             add_y(older)
-        add_pair(g, 0)
+        if g < 9:
+            add_pair(g, 0)
 
     def last_step():
+        add_pair(LAST - 1, 0)
         multiply(LAST, 0)
+        for part in range(1, PARTS):
+            multiply(LAST, part)
+            if part > 1:
+                add_pair(LAST, part - 2)
+        add_pair(LAST, PARTS - 2)
         add_z(LAST - 3)
-        multiply(LAST, 1)
-        add_pair(LAST, 0)
-        add_pair(LAST, 1)
+        add_pair(LAST, PARTS - 1)
         add_y(LAST - 6)
         add_z(LAST - 2)
+        add_y(LAST - 5)
         add_z(LAST - 1)
-        add_y(LAST - 5)
-        add_z(LAST, 0)
         add_y(LAST - 4)
-        add_z(LAST, 1)
+        for part in range(PARTS):
+            add_z(LAST, part)
         for g in range(LAST - 3, LAST):
             add_y(g)
-        add_y(LAST, 0)
-        add_y(LAST, 1)
+        for part in range(PARTS):
+            add_y(LAST, part)
 
     step(0)
     for slot in range(SLOTS):
@@ -424,7 +431,7 @@
             dma((len(UNITS),)),
         ],
         compiler_params=pltpu.CompilerParams(
-            collective_id=0, has_side_effects=True, vmem_limit_bytes=63 * 1024 * 1024
+            collective_id=0, has_side_effects=True, vmem_limit_bytes=53 * 1024 * 1024
         ),
     )(gate_input.reshape(halved), up_input.reshape(halved), down_weight)
 

time: 121 us -> 116 us (0.959)
  the two profiles are of different devices: /device:TPU:15 before, /device:TPU:8 now
where the time goes in v3:
time: 116 us
  Pallas kernels  115 us (99%)
    pallas_call x1, Pallas kernels, body(): pl.pallas_call(kernel, out_shape=jax.ShapeDtypeStruct((seqs, tokens // 2,...  115 us

profile of v3, /device:TPU:8, one launch (start us, length us, event | category | flops | bytes accessed | tf_op | source)
XLA Modules:
  0.0 115.7 jit_solution(283259053693108413)
XLA Ops:
  0.0 114.9 %shard_map.37 = bf16[2,64,2048]{2,1,0:T(8,128)(2,1)S(1)} custom-call(bf16[2,2,64,3328]{3,2,1,0:T(8,128)(2,1)} %bitcast.2, bf16[2,2,64,3328]{3,2,1,0:T(8,128)(2,1)} %bitcast.3, bf16[3328,2048]{1,0:T(8,128)(2,1)} %weight_ref.1), custom_call_target="tpu_custom_call" | custom-call | tf_op jit(solution)/shard_map/pallas_call | solution.py:400
  114.9 0.8 copy.5

commit v4 on v3

--- a/solution.py
+++ b/solution.py
@@ -11,7 +11,7 @@
 
 BLOCKS = 8
 ROWS = 16
-AHEAD = 3
+AHEAD = 4
 GROUP_SIZES = (8, 6, 6, 6, 6, 5, 6, 4, 6, 3, 3, 2, 3)
 LAST = len(GROUP_SIZES) - 1
 PARTS = 4
@@ -232,17 +232,19 @@
         size = GROUP_SIZES[g]
         span = width // PARTS if g == LAST else width
 
+        step_n = min(1024, span)
+
         def tile(n, carry):
-            columns = pl.ds(pl.multiple_of(n * TILE_N, TILE_N), TILE_N)
-            taken = pl.ds(pl.multiple_of(n * TILE_N + part * span, TILE_N), TILE_N)
+            columns = pl.ds(pl.multiple_of(n * step_n, step_n), step_n)
+            taken = pl.ds(pl.multiple_of(n * step_n + part * span, step_n), step_n)
             left = hidden[g][...].reshape(size * 2 * ROWS, -1)
             value = jnp.dot(left, weight[:, taken], preferred_element_type=jnp.float32)
-            value = value.reshape(size, 2, ROWS, TILE_N)
+            value = value.reshape(size, 2, ROWS, step_n)
             for half in range(2):
                 products(g, part, half)[:, :, columns] = value[:, half]
             return carry
 
-        lax.fori_loop(0, span // TILE_N, tile, 0)
+        lax.fori_loop(0, span // step_n, tile, 0)
         pair_copy(g, part).start()
 
     def tiles(count, span, body):

time: 116 us -> 114 us (0.983)
  Pallas kernels: 115 us -> 113 us
    pallas_call x1, Pallas kernels: 115 us -> 113 us  [body(): pl.pallas_call(kernel, out_shape=jax.ShapeDtypeStruct((seqs, tokens // 2,...]
where the time goes in v4:
time: 114 us
  Pallas kernels  113 us (99%)
    pallas_call x1, Pallas kernels, body(): pl.pallas_call(kernel, out_shape=jax.ShapeDtypeStruct((seqs, tokens // 2,...  113 us

profile of v4, /device:TPU:8, one launch (start us, length us, event | category | flops | bytes accessed | tf_op | source)
XLA Modules:
  0.0 113.9 jit_solution(11078598846313698269)
XLA Ops:
  0.0 113.1 %shard_map.37 = bf16[2,64,2048]{2,1,0:T(8,128)(2,1)S(1)} custom-call(bf16[2,2,64,3328]{3,2,1,0:T(8,128)(2,1)} %bitcast.2, bf16[2,2,64,3328]{3,2,1,0:T(8,128)(2,1)} %bitcast.3, bf16[3328,2048]{1,0:T(8,128)(2,1)} %weight_ref.1), custom_call_target="tpu_custom_call" | custom-call | tf_op jit(solution)/shard_map/pallas_call | solution.py:402
  113.1 0.8 copy.5
